TPU v7x, 16 devices: a whole 2x2x2 slice. The times are simulated.
16 devices in a mesh: tp: 4 (over z, y), dp: 4 (over x, core).
Axes of the slice: x: 2, y: 2, z: 2, core: 2. Of those that a mesh axis runs over, the one named last changes fastest.
Arguments:
- hidden: bfloat16 [4, 1024, 768], P('dp')
- ln_gamma: float32 [768], replicated
- ln_beta: float32 [768], replicated
- embed_table: bfloat16 [50304, 768], P('tp')
- labels: int32 [4, 1024], P('dp')
- loss_mask: int32 [4, 1024], P('dp')
Outputs:
- output 1: float32 [], replicated
- output 2: bfloat16 [4, 1024, 768], P('dp')
- output 3: float32 [50304, 768], P('tp')
- output 4: float32 [768], replicated
- output 5: float32 [768], replicated
All inputs are finite; a program needn't handle non-finite values.
Results may differ from a plain program's by a relative error of at most 0.001.
Values sent between devices are 32-bit elements.
A program may use at most 1 GiB of HBM per device.

v0:
```python
import jax
import jax.numpy as jnp
from jax import lax
from jax.sharding import PartitionSpec as P

LAYER_EPS = 1e-5


def layer_norm_fwd(hidden, ln_gamma, ln_beta):
    x_float = hidden.astype(jnp.float32)
    row_mean = jnp.mean(x_float, axis=-1, keepdims=True)
    centered = x_float - row_mean
    inv_std = lax.rsqrt(jnp.mean(centered * centered, axis=-1, keepdims=True) + LAYER_EPS)
    x_hat = centered * inv_std
    normed = (x_hat * ln_gamma + ln_beta).astype(jnp.bfloat16)
    return x_hat, inv_std, normed


def layer_norm_bwd(grad_normed, x_hat, inv_std, ln_gamma):
    grad_scaled = grad_normed * ln_gamma
    grad_x = (grad_scaled - jnp.mean(grad_scaled, axis=-1, keepdims=True) - x_hat * jnp.mean(grad_scaled * x_hat, axis=-1, keepdims=True)) * inv_std
    return grad_x.astype(jnp.bfloat16)


def solution(mesh):
    def local_step(hidden, ln_gamma, ln_beta, embed_shard, labels, loss_mask):
        shard_rows = embed_shard.shape[0]
        shard_start = lax.axis_index('tp') * shard_rows
        x_hat, inv_std, normed = layer_norm_fwd(hidden, ln_gamma, ln_beta)
        logits = jnp.einsum('bsd,vd->bsv', normed, embed_shard, preferred_element_type=jnp.float32)
        row_max = lax.pmax(jnp.max(logits, axis=-1, keepdims=True), 'tp')
        shifted = jnp.exp(logits - row_max)
        exp_sum = lax.psum(jnp.sum(shifted, axis=-1, keepdims=True), 'tp')
        vocab_ids = lax.broadcasted_iota(jnp.int32, (1, 1, shard_rows), 2) + shard_start
        is_target = vocab_ids == labels[..., None]
        target_logit = lax.psum(jnp.sum(jnp.where(is_target, logits, 0.0), axis=-1, keepdims=True), 'tp')
        log_norm = row_max + jnp.log(exp_sum)
        mask_float = loss_mask.astype(jnp.float32)[..., None]
        token_count = lax.psum(jnp.sum(mask_float), 'dp')
        mean_loss = lax.psum(jnp.sum(mask_float * (log_norm - target_logit)), 'dp') / token_count
        soft_probs = shifted / exp_sum
        grad_logits = (jnp.where(is_target, soft_probs - 1.0, soft_probs) * (mask_float / token_count)).astype(jnp.bfloat16)
        grad_normed = lax.psum(jnp.einsum('bsv,vd->bsd', grad_logits, embed_shard, preferred_element_type=jnp.float32), 'tp')
        d_embed = lax.psum(jnp.einsum('bsv,bsd->vd', grad_logits, normed, preferred_element_type=jnp.float32), 'dp')
        d_gamma = lax.psum(jnp.sum(grad_normed * x_hat, axis=(0, 1)), 'dp')
        d_beta = lax.psum(jnp.sum(grad_normed, axis=(0, 1)), 'dp')
        d_hidden = layer_norm_bwd(grad_normed, x_hat, inv_std, ln_gamma)
        return mean_loss, d_hidden, d_embed, d_gamma, d_beta

    return jax.shard_map(local_step, mesh=mesh, in_specs=(P('dp', None, None), P(None), P(None), P('tp', None), P('dp', None), P('dp', None)), out_specs=(P(), P('dp', None, None), P('tp', None), P(None), P(None)), check_vma=False)
```

profile of v0, /device:TPU:0, one launch (start us, length us, event | category | flops | bytes accessed | tf_op | source)
XLA Modules:
  0.0 903.4 jit_solution(16231263381876966514)
XLA Ops:
  7.2 0.0 copy-start
  7.2 0.0 copy-start.3
  7.2 0.0 copy-start.4
  7.2 0.0 all-reduce.5.cloned.1.call-start
  7.2 1.4 convert_reduce_fusion.1
  8.7 9.2 %psum.59 = f32[]{:T(128)} all-reduce(f32[]{:T(128)} %convert_reduce_fusion.1), channel_id=1, replica_groups=mesh['tp'=4,'dp'=4] {'dp'}, use_global_device_ids=true, to_apply=%region_11.12 | all-reduce | flops 1 | bytes 8 | tf_op jit(solution)/shard_map/psum | solution.py:39
  17.9 1.3 convert_divide_fusion
  19.2 1.7 convert_reduce_fusion
  20.9 2.0 fusion.17
  23.0 0.0 copy-done
  23.0 0.0 copy-done.3
  23.0 0.0 copy-done.4
  23.0 0.0 copy-start.2
  23.0 32.9 %fusion.24 = (f32[1024]{0:T(1024)S(1)}, f32[1024,12576]{0,1:T(8,128)}) fusion(bf16[12576,768]{1,0:T(8,128)(2,1)} %param.9, bf16[1,1024,768]{2,1,0:T(8,128)(2,1)S(1)} %copy-done, f32[768]{0:T(1024)S(1)} %copy-done.4, f32[768]{0:T(1024)S(1)} %copy-done.3, f32[1024]{0:T(1024)S(1)} %add_rsqrt_fusion, f32[1024]{0:T(1024)S(1)} %broadcast_multiply_fusion.2), kind=kOutput, calls=%fused_computation.37 | convolution fusion | flops 19797934080 | bytes 72419328 | tf_op jit(solution)/shard_map/bsd,vd->bsv/dot_general | solution.py:30
  55.9 10.0 %pmax.7 = f32[1,1024,1]{1,2,0:T(1,128)S(1)} all-reduce(f32[1,1024,1]{1,2,0:T(1,128)S(1)} %bitcast.31), channel_id=1, replica_groups=mesh['tp'=4,'dp'=4] {'tp'}, use_global_device_ids=true, to_apply=%region_3.0 | all-reduce | flops 1024 | bytes 8192 | tf_op jit(solution)/shard_map/pmax | solution.py:31
  65.9 0.0 copy-done.2
  65.9 22.3 %fusion.3 = (f32[1024]{0:T(1024)S(1)}, f32[1024]{0:T(1024)S(1)}) fusion(f32[1024,12576]{0,1:T(8,128)} %get-tuple-element.17, f32[1024]{0:T(1024)S(1)} %bitcast.23, s32[1024]{0:T(1024)S(1)} %bitcast.25, s32[12576]{0:T(1024)S(1)} %iota_add_fusion), kind=kLoop, calls=%fused_computation.6 | loop fusion | flops 64387072 | bytes 51577984 | tf_op jit(solution)/shard_map/reduce_sum | solution.py:33
  88.1 8.3 all-reduce.1
  96.4 26.3 %fusion.2 = bf16[1024,12576]{0,1:T(8,128)(2,1)} fusion(f32[1024,12576]{0,1:T(8,128)} %get-tuple-element.17, f32[1024]{0:T(1024)S(1)} %bitcast.27, f32[1024]{0:T(1024)S(1)} %bitcast.30, s32[1024]{0:T(1024)S(1)} %bitcast.26, f32[1024]{0:T(1024)S(1)} %bitcast.24, s32[12576]{0:T(1024)S(1)} %iota_add_fusion), kind=kLoop, calls=%fused_computation.4 | loop fusion | flops 90144768 | bytes 77333632 | tf_op jit(solution)/shard_map/convert_element_type | solution.py:42
  122.7 27.9 %convolution_bitcast_fusion = f32[1,1024,768]{2,1,0:T(8,128)} fusion(bf16[1024,12576]{0,1:T(8,128)(2,1)} %fusion.2, bf16[12576,768]{1,0:T(8,128)(2,1)} %param.9), kind=kOutput, calls=%fused_computation.24 | convolution fusion | flops 19780337664 | bytes 48218112 | tf_op jit(solution)/shard_map/bsv,vd->bsd/dot_general | solution.py:43
  150.6 0.0 all-reduce.5.cloned.1.call-update
  150.6 0.3 all-reduce.7.cloned.1.call-start
  150.9 30.7 %fusion.20 = f32[12576,768]{1,0:T(8,128)} fusion(bf16[1024,12576]{0,1:T(8,128)(2,1)} %fusion.2, bf16[1,1024,768]{2,1,0:T(8,128)(2,1)S(1)} %copy-done, f32[768]{0:T(1024)S(1)} %copy-done.4, f32[768]{0:T(1024)S(1)} %copy-done.3, f32[1024]{0:T(1024)S(1)} %add_rsqrt_fusion, f32[1024]{0:T(1024)S(1)} %broadcast_multiply_fusion.2), kind=kOutput, calls=%fused_computation.35 | convolution fusion | flops 19785056256 | bytes 65976320 | tf_op jit(solution)/shard_map/bsv,bsd->vd/dot_general | solution.py:44
  181.6 0.0 all-reduce.7.cloned.1.call-update
  181.6 0.7 copy-done.1
  182.3 0.6 fusion.19
  182.9 46.0 %all-reduce.5.cloned.1.call-done = f32[1,1024,768]{2,1,0:T(8,128)} async-done(((f32[1,1024,768]{2,1,0:T(8,128)}), f32[1,1024,768]{2,1,0:T(8,128)}) %all-reduce.5.cloned.1.call-update) | async-done | bytes 3145744 | tf_op jit(solution)/shard_map/psum | solution.py:43
  228.9 3.1 fusion.16
  231.9 7.5 all-reduce
  240.8 3.5 fusion.15
  244.3 623.8 %all-reduce.7.cloned.1.call-done = f32[12576,768]{1,0:T(8,128)} async-done(((f32[12576,768]{1,0:T(8,128)}), f32[12576,768]{1,0:T(8,128)}) %all-reduce.7.cloned.1.call-update) | async-done | bytes 38633488 | tf_op jit(solution)/shard_map/psum | solution.py:44
  868.1 27.3 %copy.13 = f32[12576,768]{1,0:T(8,128)} copy(f32[12576,768]{1,0:T(8,128)} %all-reduce.7.cloned.1.call-done) | data formatting | bytes 77266944
  (5 shorter events, 0.0 us)
Async XLA Ops:
  7.2 15.8 %copy-start = (bf16[1,1024,768]{2,1,0:T(8,128)(2,1)S(1)}, bf16[1,1024,768]{2,1,0:T(8,128)(2,1)}, u32[]{:S(2)}) copy-start(bf16[1,1024,768]{2,1,0:T(8,128)(2,1)} %param.6) | copy-start | bytes 4718596
  7.2 15.8 %copy-start.3 = (f32[768]{0:T(1024)S(1)}, f32[768]{0:T(1024)}, u32[]{:S(2)}) copy-start(f32[768]{0:T(1024)} %param.7) | copy-start | bytes 9220
  7.2 15.8 %copy-start.4 = (f32[768]{0:T(1024)S(1)}, f32[768]{0:T(1024)}, u32[]{:S(2)}) copy-start(f32[768]{0:T(1024)} %param.8) | copy-start | bytes 9220
  7.2 221.7 %all-reduce.5.cloned.1.call-start = ((), (), s32[]{:S(2)}) async-start(), calls=%async_computation | async-start | bytes 6291456 | tf_op jit(solution)/shard_map/psum | solution.py:43
  23.0 42.9 %copy-start.2 = (s32[1,1024]{1,0:T(1,128)S(1)}, s32[1,1024]{1,0:T(1,128)}, u32[]{:S(2)}) copy-start(s32[1,1024]{1,0:T(1,128)} %param.10) | copy-start | bytes 12292
  150.6 717.5 %all-reduce.7.cloned.1.call-start = ((), (), s32[]{:S(2)}) async-start(), calls=%async_computation.1 | async-start | bytes 77266944 | tf_op jit(solution)/shard_map/psum | solution.py:44
  181.6 0.7 copy-start.1
Sparse Core Ops, SparseCore 0:
  150.7 78.1 all-reduce.4
  232.0 636.1 all-reduce.6
where the time goes:
time: 904 us; the launch traced here: 903 us
  waiting for transfers between devices  670 us (74%)
  matrix products  91.5 us (10%)
  other arithmetic  62.1 us (7%)
  blocking collectives  35 us (4%)
  local copies, waits for them, and re-layouts  28 us (3%)
  between operations  16.6 us (2%)
    psum x1, waiting for transfers between devices, local_step(): lax.psum(jnp.einsum('bsv,bsd->vd', grad_logits, normed, preferred_element...  624 us
    psum x1, waiting for transfers between devices, local_step(): lax.psum(jnp.einsum('bsv,vd->bsd', grad_logits, embed_shard, preferred_el...  46 us
    dot_general x1, matrix products, local_step(): jnp.einsum('bsd,vd->bsv', normed, embed_shard, preferred_element_type=jnp...  32.9 us
    dot_general x1, matrix products, local_step(): jnp.einsum('bsv,bsd->vd', grad_logits, normed, preferred_element_type=jnp...  30.7 us
    unnamed x11, local copies, waits for them, and re-layouts  28 us
    dot_general x1, matrix products, local_step(): jnp.einsum('bsv,vd->bsd', grad_logits, embed_shard, preferred_element_typ...  27.9 us
    convert_element_type x1, other arithmetic, local_step(): (jnp.where(is_target, soft_probs - 1.0, soft_probs) * (mask_float / token...  26.3 us
    reduce_sum x1, other arithmetic, local_step(): exp_sum = lax.psum(jnp.sum(shifted, axis=-1, keepdims=True), 'tp')  22.3 us
  transfers between devices with their start and end apart: 2, of which 2 were waited for; matrix products, arithmetic and copies ran while one was open for 4% of the time, Pallas kernels for 0%

commit v1 on v0

v1 whole, which is shorter than its diff:
```python
import functools

import jax
import jax.numpy as jnp
from jax import lax
from jax.experimental import pallas as pl
from jax.experimental.pallas import tpu as pltpu
from jax.sharding import PartitionSpec as P

LAYER_EPS = 1e-5
BLOCK = 256
PAIR = 2 * BLOCK
BIG = 1e30
VMEM_LIMIT = 62 * 1024 * 1024


def chunk_list(total, size):
    return [(start, min(size, total - start)) for start in range(0, total, size)]


def logits_kernel(idx_ref, e_ref, za_ref, zb_ref, *rest):
    l_ref, zc_ref, st_ref = rest[-3:]
    pl.when(pl.program_id(0) < idx_ref[1])(lambda: logits_step(e_ref, za_ref, zb_ref, l_ref, zc_ref, st_ref))


def logits_step(e_ref, za_ref, zb_ref, l_ref, zc_ref, st_ref):
    zc_ref[0, :BLOCK, :] = za_ref[0]
    zc_ref[0, BLOCK:, :] = zb_ref[0]
    rows = e_ref.shape[0]
    size = 528
    full = rows // size

    def step(start, n, carry):
        top, total = carry
        tile = lax.dot_general(e_ref[pl.ds(start, n), :], zc_ref[0], (((1,), (1,)), ((), ())), preferred_element_type=jnp.float32)
        l_ref[0, pl.ds(start, n), :] = tile
        new_top = jnp.maximum(top, jnp.max(tile, axis=0, keepdims=True))
        total = total * jnp.exp(top - new_top) + jnp.sum(jnp.exp(tile - new_top), axis=0, keepdims=True)
        return new_top, total

    carry = (jnp.full((1, PAIR), -BIG, jnp.float32), jnp.zeros((1, PAIR), jnp.float32))
    carry = lax.fori_loop(0, full, lambda i, c: step(pl.multiple_of(i * size, 16), size, c), carry)
    if rows > full * size:
        carry = step(full * size, rows - full * size, carry)
    st_ref[0, 0:1, :] = carry[0]
    st_ref[0, 1:2, :] = carry[1]


def grad_tile(tile, lse, weight, is_target):
    probs = jnp.exp(tile - lse)
    return (jnp.where(is_target, probs - 1.0, probs) * weight).astype(jnp.bfloat16)


def dz_kernel(idx_ref, *refs):
    pl.when(pl.program_id(0) < idx_ref[1])(lambda: dz_step(idx_ref, *refs))


def dz_step(idx_ref, e_ref, l_ref, tok_ref, lab_ref, dz_ref, tl_ref, acc_ref, sem):
    i = pl.program_id(0)
    rows = e_ref.shape[0]
    size = 512
    full = rows // size
    lse = tok_ref[0, 0:1, :]
    weight = tok_ref[0, 1:2, :]
    label = lab_ref[0]
    acc_ref[...] = jnp.zeros_like(acc_ref)

    def step(start, n, target):
        tile = l_ref[0, pl.ds(start, n), :]
        is_target = lax.broadcasted_iota(jnp.int32, (n, PAIR), 0) == label - start
        target = target + jnp.sum(jnp.where(is_target, tile, 0.0), axis=0, keepdims=True)
        grad = grad_tile(tile, lse, weight, is_target)
        acc_ref[...] += lax.dot_general(grad, e_ref[pl.ds(start, n), :], (((0,), (0,)), ((), ())), preferred_element_type=jnp.float32)
        return target

    target = lax.fori_loop(0, full, lambda k, c: step(pl.multiple_of(k * size, 16), size, c), jnp.zeros((1, PAIR), jnp.float32))
    if rows > full * size:
        target = step(full * size, rows - full * size, target)
    tl_ref[0] = target
    copies = [pltpu.make_async_copy(acc_ref.at[pl.ds(h * BLOCK, BLOCK), :], dz_ref.at[idx_ref[2 + 2 * i + h]], sem.at[h]) for h in range(2)]
    for copy in copies:
        copy.start()
    for copy in copies:
        copy.wait()


def de_kernel(idx_ref, l_ref, z_ref, tok_ref, lab_ref, de_ref):
    j, i = pl.program_id(0), pl.program_id(1)
    rows = de_ref.shape[0]
    lse = tok_ref[0, 0:1, :]
    weight = tok_ref[0, 1:2, :]
    label = lab_ref[0] - j * rows

    def fill(first):
        for start, n in chunk_list(rows, 528):
            is_target = lax.broadcasted_iota(jnp.int32, (n, PAIR), 0) == label - start
            grad = grad_tile(l_ref[0, start:start + n, :], lse, weight, is_target)
            part = jnp.dot(grad, z_ref[0], preferred_element_type=jnp.float32)
            if first:
                de_ref[start:start + n, :] = part
            else:
                de_ref[start:start + n, :] += part

    pl.when(i == 0)(lambda: fill(True))
    pl.when((i > 0) & (i < idx_ref[1]))(lambda: fill(False))


def order_blocks(active):
    n = active.shape[0]
    act = active.astype(jnp.int32)
    ids = jnp.arange(n, dtype=jnp.int32)
    before = (ids[None, :] < ids[:, None]).astype(jnp.int32)
    ahead = jnp.sum(before * act[None, :], axis=1)
    count = jnp.sum(act)
    place = jnp.where(act > 0, ahead, count + ids - ahead)
    order = jnp.sum(jnp.where(place[None, :] == ids[:, None], ids[None, :], 0), axis=1)
    return order, count


def last(i, s):
    return jnp.minimum(i, s[1] - 1)


def call_logits(idx, e, z, previous, rows):
    pairs = 8
    base = 0 if previous is None else pairs // 2
    width = e.shape[1]
    extra = [] if previous is None else list(previous)
    spec = pltpu.PrefetchScalarGridSpec(
        num_scalar_prefetch=1,
        grid=(4,),
        in_specs=[
            pl.BlockSpec((rows, width), lambda i, s: (s[0], 0), pipeline_mode=pl.Buffered(1)),
            pl.BlockSpec((1, BLOCK, width), lambda i, s: (s[2 + 2 * last(i, s)], 0, 0)),
            pl.BlockSpec((1, BLOCK, width), lambda i, s: (s[3 + 2 * last(i, s)], 0, 0)),
        ] + [pl.BlockSpec(memory_space=pl.ANY)] * len(extra),
        out_specs=[
            pl.BlockSpec((1, rows, PAIR), lambda i, s: (base + last(i, s), 0, 0)),
            pl.BlockSpec((1, PAIR, width), lambda i, s: (base + last(i, s), 0, 0)),
            pl.BlockSpec((1, 2, PAIR), lambda i, s: (base + last(i, s), 0, 0)),
        ],
    )
    return pl.pallas_call(
        logits_kernel,
        grid_spec=spec,
        out_shape=[
            jax.ShapeDtypeStruct((pairs, rows, PAIR), jnp.float32),
            jax.ShapeDtypeStruct((pairs, PAIR, width), jnp.bfloat16),
            jax.ShapeDtypeStruct((pairs, 2, PAIR), jnp.float32),
        ],
        input_output_aliases={} if previous is None else {4: 0, 5: 1, 6: 2},
        compiler_params=pltpu.CompilerParams(vmem_limit_bytes=VMEM_LIMIT, dimension_semantics=("arbitrary",)),
        cost_estimate=pl.CostEstimate(flops=2 * 1200 * rows * width, bytes_accessed=4 * 1200 * rows, transcendentals=1200 * rows),
        name="logits_near" if previous is None else "logits_far",
    )(idx, e, z, z, *extra)


def call_dz(idx, e, l, tok, lab, rows):
    width = e.shape[1]
    spec = pltpu.PrefetchScalarGridSpec(
        num_scalar_prefetch=1,
        grid=(4,),
        in_specs=[
            pl.BlockSpec((rows, width), lambda i, s: (s[0], 0), pipeline_mode=pl.Buffered(1)),
            pl.BlockSpec((1, rows, PAIR), lambda i, s: (last(i, s), 0, 0)),
            pl.BlockSpec((1, 2, PAIR), lambda i, s: (last(i, s), 0, 0)),
            pl.BlockSpec((1, 1, PAIR), lambda i, s: (last(i, s), 0, 0)),
        ],
        out_specs=[
            pl.BlockSpec(memory_space=pl.ANY),
            pl.BlockSpec((1, 1, PAIR), lambda i, s: (last(i, s), 0, 0)),
        ],
        scratch_shapes=[pltpu.VMEM((PAIR, width), jnp.float32), pltpu.SemaphoreType.DMA((2,))],
    )
    return pl.pallas_call(
        dz_kernel,
        grid_spec=spec,
        out_shape=[jax.ShapeDtypeStruct((8, BLOCK, width), jnp.float32), jax.ShapeDtypeStruct((4, 1, PAIR), jnp.float32)],
        compiler_params=pltpu.CompilerParams(vmem_limit_bytes=VMEM_LIMIT, dimension_semantics=("arbitrary",)),
        cost_estimate=pl.CostEstimate(flops=2 * 1200 * rows * width, bytes_accessed=4 * 1200 * rows, transcendentals=1200 * rows),
        name="dz_part",
    )(idx, e, l, tok, lab)


def call_de(idx, l, zc, tok, lab):
    rows, width = l.shape[1], zc.shape[2]
    splits = 3
    part = rows // splits
    spec = pltpu.PrefetchScalarGridSpec(
        num_scalar_prefetch=1,
        grid=(splits, 8),
        in_specs=[
            pl.BlockSpec((1, part, PAIR), lambda j, i, s: (s[2 + last(i, s)], j, 0)),
            pl.BlockSpec((1, PAIR, width), lambda j, i, s: (s[2 + last(i, s)], 0, 0)),
            pl.BlockSpec((1, 2, PAIR), lambda j, i, s: (s[2 + last(i, s)], 0, 0)),
            pl.BlockSpec((1, 1, PAIR), lambda j, i, s: (s[2 + last(i, s)], 0, 0)),
        ],
        out_specs=pl.BlockSpec((part, width), lambda j, i, s: (j, 0)),
    )
    return pl.pallas_call(
        de_kernel,
        grid_spec=spec,
        out_shape=jax.ShapeDtypeStruct((rows, width), jnp.float32),
        compiler_params=pltpu.CompilerParams(vmem_limit_bytes=VMEM_LIMIT, dimension_semantics=("arbitrary", "arbitrary")),
        cost_estimate=pl.CostEstimate(flops=2 * 2400 * rows * width, bytes_accessed=4 * 2400 * rows, transcendentals=2400 * rows),
        name="de_part",
    )(idx, l, zc, tok, lab)


def solution(mesh):
    n_tp, n_dp = mesh.shape['tp'], mesh.shape['dp']

    def flip(x, axis, bits):
        n = n_tp if axis == 'tp' else n_dp
        return lax.ppermute(x, axis, [(k, k ^ bits) for k in range(n)])

    def pick(x, index):
        return lax.dynamic_index_in_dim(x, index, 0, keepdims=False)

    def local_step(hidden, ln_gamma, ln_beta, embed_shard, labels, loss_mask):
        tp, dp = lax.axis_index('tp'), lax.axis_index('dp')
        core, side = dp % 2, dp // 2
        seq, width = hidden.shape[1:]
        quarters = seq // BLOCK
        rows = embed_shard.shape[0] // 2
        row_start = tp * (2 * rows) + core * rows

        x_float = hidden[0].astype(jnp.float32)
        centered = x_float - jnp.mean(x_float, axis=-1, keepdims=True)
        inv_std = lax.rsqrt(jnp.mean(centered * centered, axis=-1, keepdims=True) + LAYER_EPS)
        x_hat = centered * inv_std

        def to_z(values):
            return (values * ln_gamma + ln_beta).astype(jnp.bfloat16)

        marked = jnp.where(loss_mask[0] > 0, labels[0], -1)
        marked = lax.all_gather(marked, 'dp').reshape(n_dp, quarters, BLOCK)
        token_count = jnp.sum((marked >= 0).astype(jnp.float32))
        near = lax.dynamic_slice_in_dim(marked, side * 2, 2, 0).reshape(2 * quarters, BLOCK)
        far = lax.dynamic_slice_in_dim(marked, (1 - side) * 2, 2, 0).reshape(2 * quarters, BLOCK)
        near_order, near_n = order_blocks(jnp.any(near >= 0, axis=1))
        far_order, far_n = order_blocks(jnp.any(far >= 0, axis=1))
        near_pairs, far_pairs = (near_n + 1) // 2, (far_n + 1) // 2
        lab = jnp.concatenate([near[near_order], far[far_order]]).reshape(8, 1, PAIR)
        core_id = core.astype(jnp.int32)[None]
        near_idx = jnp.concatenate([core_id, near_pairs[None], near_order])
        far_idx = jnp.concatenate([core_id, far_pairs[None], (far_order // quarters) * quarters + ((far_order % quarters) ^ tp)])
        pair_ids = jnp.arange(8, dtype=jnp.int32)
        pair_idx = jnp.where(pair_ids < near_pairs, pair_ids, jnp.minimum(4 + pair_ids - near_pairs, 7))
        pair_idx = jnp.concatenate([core_id, (near_pairs + far_pairs)[None], pair_idx])

        own_quarter = pick(x_hat.reshape(quarters, BLOCK, width), tp)
        mate = flip(x_hat, 'dp', 1)
        first_piece = flip(own_quarter, 'dp', 2)
        pieces = [first_piece] + [flip(first_piece, 'tp', k) for k in (1, 2, 3)]
        mate_pieces = [flip(piece, 'dp', 1) for piece in pieces]

        def by_core(mine, other):
            return jnp.stack([jnp.where(core == 0, mine, other), jnp.where(core == 0, other, mine)])

        near_z = to_z(by_core(x_hat, mate)).reshape(2 * quarters, BLOCK, width)
        previous = call_logits(near_idx, embed_shard, near_z, None, rows)
        far_z = to_z(by_core(jnp.stack(pieces), jnp.stack(mate_pieces))).reshape(2 * quarters, BLOCK, width)
        logits, z_pairs, stats = call_logits(far_idx, embed_shard, far_z, previous, rows)

        every = lax.all_gather(stats, ('tp', 'dp')).reshape(n_tp, 2, 2, 8, 2, PAIR)
        every = lax.dynamic_index_in_dim(every, side, 1, keepdims=False).reshape(2 * n_tp, 8, 2, PAIR)
        top = jnp.max(every[:, :, 0], axis=0)
        total = jnp.sum(every[:, :, 1] * jnp.exp(every[:, :, 0] - top), axis=0)
        live = lab[:, 0] >= 0
        lse = jnp.where(live, top + jnp.log(total), BIG)
        tok = jnp.stack([lse, jnp.where(live, 1.0 / token_count, 0.0)], axis=1)
        local_lab = lab - row_start

        dz, target = call_dz(near_idx, embed_shard, logits, tok, local_lab, rows)
        d_rows = call_de(pair_idx, logits, z_pairs, tok, local_lab)
        d_mate = flip(d_rows, 'dp', 1)
        d_embed = by_core(d_rows, d_mate).reshape(2 * rows, width)

        dz = jnp.where((near >= 0)[..., None], dz, 0.0).reshape(2, quarters, BLOCK, width)
        part = pick(dz, core) + flip(pick(dz, 1 - core), 'dp', 1)
        grad = pick(part, tp)
        for k in (1, 2, 3):
            grad = grad + flip(pick(part, tp ^ k), 'tp', k)
        hat = own_quarter
        d_gamma = jnp.sum(grad * hat, axis=0)
        d_beta = jnp.sum(grad, axis=0)
        scaled = grad * ln_gamma
        inner = scaled - jnp.mean(scaled, axis=-1, keepdims=True) - hat * jnp.mean(scaled * hat, axis=-1, keepdims=True)
        inner = jnp.stack([inner] + [flip(inner, 'tp', k) for k in (1, 2, 3)])
        inner = jnp.stack([pick(inner, tp ^ q) for q in range(quarters)]).reshape(seq, width)
        d_hidden = (inner * inv_std).astype(jnp.bfloat16)[None]

        near_live = live[:4]
        lead = ((tp == 0) & (core == 0)).astype(jnp.float32)
        loss = jnp.sum(jnp.where(near_live, lead * lse[:4] - target[:, 0], 0.0)) / token_count
        sums = lax.psum(jnp.concatenate([d_gamma, d_beta, jnp.broadcast_to(loss, (128,))]), ('tp', 'dp'))
        return sums[2 * width], d_hidden, d_embed, sums[:width], sums[width:2 * width]

    return jax.shard_map(local_step, mesh=mesh, in_specs=(P('dp', None, None), P(None), P(None), P('tp', None), P('dp', None), P('dp', None)), out_specs=(P(), P('dp', None, None), P('tp', None), P(None), P(None)), check_vma=False)
```

time: 904 us -> 472 us (0.52)
  waiting for transfers between devices: 670 us -> 72.2 us
  Pallas kernels: 0 us -> 204 us
  matrix products: 91.5 us -> 0 us
  blocking collectives: 35 us -> 99.6 us
  local copies, waits for them, and re-layouts: 28 us -> 6.94 us
  other arithmetic: 62.1 us -> 78.2 us
  starting transfers between devices: 0.3 us -> 14.8 us
  between operations: 16.6 us -> 4.54 us
    psum x2 -> x0, waiting for transfers between devices: 670 us -> none  [the longest x1 624 us: local_step(): lax.psum(jnp.einsum('bsv,bsd->vd', grad_logits, normed, preferred_element...]
    pallas_call x0 -> x4, Pallas kernels: none -> 204 us  [the longest x2 93.1 us: call_logits(): pl.pallas_call(logits_kernel, grid_spec=spec, out_shape=[jax.ShapeDtypeSt...]
    dot_general x3 -> x0, matrix products: 91.5 us -> none  [the longest x1 32.9 us: local_step(): jnp.einsum('bsd,vd->bsv', normed, embed_shard, preferred_element_type=jnp...]
    ppermute x0 -> x17, waiting for transfers between devices: none -> 72.2 us  [flip(): return lax.ppermute(x, axis, [(k, k ^ bits) for k in range(n)])]
    another operation x0 -> x8, other arithmetic: none -> 46.2 us  [the longest x5 44.9 us: by_core(): jnp.stack([jnp.where(core == 0, mine, other), jnp.where(core == 0, other,...]
    psum x3 -> x1, blocking collectives: 25 us -> 69.3 us  [local_step(): lax.psum(jnp.concatenate([d_gamma, d_beta, jnp.broadcast_to(loss, (128,))...]
    all_gather x0 -> x2, blocking collectives: none -> 30.3 us  [the longest x1 16.4 us: local_step(): marked = lax.all_gather(marked, 'dp').reshape(n_dp, quarters, BLOCK)]
    unnamed x11 -> x29, local copies, waits for them, and re-layouts: 28 us -> 2.98 us
  transfers between devices with their start and end apart: 2 -> 17, of which waited for: 2 -> 5; matrix products, arithmetic and copies ran while one was open for 4% -> 5% of each run, Pallas kernels for 0% -> 10%
where the time goes in v1:
time: 472 us; the launch traced here: 480 us
  Pallas kernels  204 us (43%)
  blocking collectives  99.6 us (21%)
  other arithmetic  78.2 us (17%)
  waiting for transfers between devices  72.2 us (15%)
  starting transfers between devices  14.8 us (3%)
  local copies, waits for them, and re-layouts  6.94 us (1%)
    pallas_call x2, Pallas kernels, call_logits(): pl.pallas_call(logits_kernel, grid_spec=spec, out_shape=[jax.ShapeDtypeSt...  93.1 us
    ppermute x17, waiting for transfers between devices, flip(): return lax.ppermute(x, axis, [(k, k ^ bits) for k in range(n)])  72.2 us
    psum x1, blocking collectives, local_step(): lax.psum(jnp.concatenate([d_gamma, d_beta, jnp.broadcast_to(loss, (128,))...  69.3 us
    pallas_call x1, Pallas kernels, call_de(): pl.pallas_call(de_kernel, grid_spec=spec, out_shape=jax.ShapeDtypeStruct(...  62 us
    pallas_call x1, Pallas kernels, call_dz(): pl.pallas_call(dz_kernel, grid_spec=spec, out_shape=[jax.ShapeDtypeStruct...  48.6 us
    another operation x5, other arithmetic, by_core(): jnp.stack([jnp.where(core == 0, mine, other), jnp.where(core == 0, other,...  44.9 us
    all_gather x1, blocking collectives, local_step(): marked = lax.all_gather(marked, 'dp').reshape(n_dp, quarters, BLOCK)  16.4 us
    ppermute x17, starting transfers between devices, flip(): return lax.ppermute(x, axis, [(k, k ^ bits) for k in range(n)])  14.8 us
  transfers between devices with their start and end apart: 17, of which 5 were waited for; matrix products, arithmetic and copies ran while one was open for 5% of the time, Pallas kernels for 10%

profile of v1, /device:TPU:0, one launch (start us, length us, event | category | flops | bytes accessed | tf_op | source)
XLA Modules:
  0.0 480.1 jit_solution(5311478636803557189)
XLA Ops:
  0.6 1.8 convert_reduce_fusion
  2.5 2.0 multiply_reduce_fusion
  4.5 2.0 convert.5
  6.5 2.2 fusion.7
  8.7 3.2 collective-permute-start
  11.9 2.1 fusion.3
  14.1 16.4 %all-gather.1 = s32[4,1,1024]{2,1,0:T(1,128)S(1)} all-gather(s32[1,1,1024]{2,1,0:T(1,128)S(1)} %fusion.18), channel_id=1, replica_groups=mesh['tp'=4,'dp'=4] {'dp'}, dimensions={0}, use_global_device_ids=true | all-gather | bytes 20480 | tf_op jit(solution)/shard_map/all_gather | solution.py:237
  35.9 1.8 collective-permute-start.1
  37.7 1.6 collective-permute-start.2
  40.7 15.6 %collective-permute-done.1 = f32[256,768]{1,0:T(8,128)} collective-permute-done((f32[256,768]{1,0:T(8,128)S(1)}, f32[256,768]{1,0:T(8,128)}, u32[]{:S(2)}, u32[]{:S(2)}) %collective-permute-start.1) | collective-permute-done | bytes 786464 | tf_op jit(solution)/shard_map/ppermute | solution.py:215
  56.3 17.7 %collective-permute-done.2 = f32[256,768]{1,0:T(8,128)} collective-permute-done((f32[256,768]{1,0:T(8,128)S(1)}, f32[256,768]{1,0:T(8,128)}, u32[]{:S(2)}, u32[]{:S(2)}) %collective-permute-start.2) | collective-permute-done | bytes 786464 | tf_op jit(solution)/shard_map/ppermute | solution.py:215
  77.7 2.9 fusion.5
  81.3 2.5 select_bitcast_fusion.3
  84.5 4.2 add_convert_fusion
  88.7 41.3 %logits_near.1 = (f32[8,6288,512]{2,1,0:T(8,128)}, bf16[8,512,768]{2,1,0:T(8,128)(2,1)}, f32[8,2,512]{2,1,0:T(2,128)}) custom-call(s32[10]{0:T(128)} %pad_add_fusion.idx_ref, bf16[12576,768]{1,0:T(8,128)(2,1)} %refs_0_.1, bf16[8,256,768]{2,1,0:T(8,128)(2,1)} %get-tuple-element.49.za_ref.zb_ref, bf16[8,256,768]{2,1,0:T(8,128)(2,1)} %get-tuple-element.49.za_ref.zb_ref), custom_call_target="tpu_custom_call" | custom-call | flops 11590041600 | bytes 30182400 | tf_op jit(solution)/shard_map/logits_near/pallas_call | solution.py:143
  130.1 51.8 %logits_far.1 = (f32[8,6288,512]{2,1,0:T(8,128)}, bf16[8,512,768]{2,1,0:T(8,128)(2,1)}, f32[8,2,512]{2,1,0:T(2,128)}) custom-call(s32[10]{0:T(128)} %pad_add_fusion.1.idx_ref, bf16[12576,768]{1,0:T(8,128)(2,1)} %refs_0_.1, bf16[8,256,768]{2,1,0:T(8,128)(2,1)} %get-tuple-element.50.za_ref.zb_ref, ...), custom_call_target="tpu_custom_call", output_to_operand_aliasing={{0}: (4, {}), {1}: (5, {}), {2}: (6, {})} | custom-call | flops 11590041600 | bytes 30182400 | tf_op jit(solution)/shard_map/logits_far/pallas_call | solution.py:143
  181.9 13.9 %all-gather = f32[128,2,512]{2,1,0:T(2,128)S(1)} all-gather(f32[8,2,512]{2,1,0:T(2,128)} %get-tuple-element.17), channel_id=2, replica_groups=mesh['tp'=4,'dp'=4] {'tp','dp'}, dimensions={0}, use_global_device_ids=true | all-gather | bytes 557056 | tf_op jit(solution)/shard_map/all_gather | solution.py:266
  196.7 62.0 %de_part.1 = f32[6288,768]{1,0:T(8,128)} custom-call(s32[10]{0:T(128)} %pad_add_fusion.2.idx_ref, f32[8,6288,512]{2,1,0:T(8,128)} %get-tuple-element.16.refs_1_.l_ref, bf16[8,512,768]{2,1,0:T(8,128)(2,1)} %get-tuple-element.20.z_ref, f32[8,2,512]{2,1,0:T(2,128)} %pad_maximum_fusion.7.refs_2_.tok_ref, s32[8,1,512]{2,1,0:T(1,128)} %sub.96.refs_3_.lab_ref), custom_call_target="tpu_custom_call" | custom-call | flops 23180083200 | bytes 60364800 | tf_op jit(solution)/shard_map/de_part/pallas_call | solution.py:200
  259.1 48.6 %dz_part.1 = (f32[8,256,768]{2,1,0:T(8,128)}, f32[4,1,512]{2,1,0:T(1,128)}) custom-call(s32[10]{0:T(128)} %pad_add_fusion.idx_ref, bf16[12576,768]{1,0:T(8,128)(2,1)} %refs_0_.1, f32[8,6288,512]{2,1,0:T(8,128)} %get-tuple-element.16.refs_1_.l_ref, f32[8,2,512]{2,1,0:T(2,128)} %pad_maximum_fusion.7.refs_2_.tok_ref, s32[8,1,512]{2,1,0:T(1,128)} %sub.96.refs_3_.lab_ref), custom_call_target="tpu_custom_call" | custom-call | flops 11590041600 | bytes 30182400 | tf_op jit(solution)/shard_map/dz_part/pallas_call | solution.py:175
  307.7 3.2 broadcast_select_fusion
  310.9 2.7 copy-done.1
  314.0 5.5 %collective-permute-done.9 = f32[4,256,768]{2,1,0:T(8,128)} collective-permute-done((f32[4,256,768]{2,1,0:T(8,128)S(1)}, f32[4,256,768]{2,1,0:T(8,128)}, u32[]{:S(2)}, u32[]{:S(2)}) %collective-permute-start.9) | collective-permute-done | bytes 3145760 | tf_op jit(solution)/shard_map/ppermute | solution.py:215
  319.4 3.2 bitcast_add_fusion
  323.5 1.4 collective-permute-start.11
  324.9 1.5 collective-permute-start.12
  326.4 16.9 %collective-permute-done.10 = f32[256,768]{1,0:T(8,128)S(1)} collective-permute-done((f32[256,768]{1,0:T(8,128)S(1)}, f32[256,768]{1,0:T(8,128)S(1)}, u32[]{:S(2)}, u32[]{:S(2)}) %collective-permute-start.10) | collective-permute-done | bytes 786464 | tf_op jit(solution)/shard_map/ppermute | solution.py:215
  343.3 16.4 %collective-permute-done.11 = f32[256,768]{1,0:T(8,128)S(1)} collective-permute-done((f32[256,768]{1,0:T(8,128)S(1)}, f32[256,768]{1,0:T(8,128)S(1)}, u32[]{:S(2)}, u32[]{:S(2)}) %collective-permute-start.11) | collective-permute-done | bytes 786464 | tf_op jit(solution)/shard_map/ppermute | solution.py:215
  360.6 1.4 collective-permute-start.13
  362.6 1.5 collective-permute-start.15
  366.1 69.3 %psum.7 = f32[1664]{0:T(1024)S(1)} all-reduce(f32[1664]{0:T(1024)S(1)} %pad_maximum_fusion.8), channel_id=1, replica_groups=mesh['tp'=4,'dp'=4] {'tp','dp'}, use_global_device_ids=true, to_apply=%region_16.17 | all-reduce | flops 1664 | bytes 13312 | tf_op jit(solution)/shard_map/psum | solution.py:297
  438.8 20.0 %select_bitcast_fusion.1 = (f32[1,6288,768]{2,1,0:T(8,128)S(1)}, f32[1,6288,768]{2,1,0:T(8,128)}) fusion(f32[6288,768]{1,0:T(8,128)} %de_part.1, f32[6288,768]{1,0:T(8,128)} %collective-permute-done.16, pred[]{:T(512)S(6)} %eq.20), kind=kLoop, calls=%fused_computation.4 | loop fusion | flops 9658368 | bytes 77266944 | tf_op jit(solution)/shard_map/stack | solution.py:259
  458.8 21.3 %pad_maximum_fusion = f32[2,6288,768]{2,1,0:T(8,128)} fusion(f32[1,6288,768]{2,1,0:T(8,128)} %get-tuple-element.31, f32[1,6288,768]{2,1,0:T(8,128)S(1)} %get-tuple-element.30), kind=kLoop, calls=%fused_computation.2 | loop fusion | flops 9658368 | bytes 77266944 | tf_op jit(solution)/shard_map/stack | solution.py:259
  (119 shorter events, 17.7 us)
Async XLA Ops:
  0.6 3.9 copy-start
  6.5 7.6 %copy-start.6 = (f32[1,256]{1,0:T(1,128)}, f32[1,256]{1,0:T(1,128)S(1)}, u32[]{:S(2)}) copy-start(f32[1,256]{1,0:T(1,128)S(1)} %get-tuple-element.53) | copy-start | bytes 3076
  6.5 7.6 %copy-start.8 = (f32[1,256]{1,0:T(1,128)}, f32[1,256]{1,0:T(1,128)S(1)}, u32[]{:S(2)}) copy-start(f32[1,256]{1,0:T(1,128)S(1)} %get-tuple-element.54) | copy-start | bytes 3076
  6.5 7.6 %copy-start.11 = (s32[1,1024]{1,0:T(1,128)S(1)}, s32[1,1024]{1,0:T(1,128)}, u32[]{:S(2)}) copy-start(s32[1,1024]{1,0:T(1,128)} %param.10) | copy-start | bytes 12292
  6.5 7.6 %copy-start.12 = (s32[1,1024]{1,0:T(1,128)S(1)}, s32[1,1024]{1,0:T(1,128)}, u32[]{:S(2)}) copy-start(s32[1,1024]{1,0:T(1,128)} %param.11) | copy-start | bytes 12292
  8.7 27.2 %collective-permute-start = (f32[256,768]{1,0:T(8,128)}, f32[256,768]{1,0:T(8,128)S(1)}, u32[]{:S(2)}, u32[]{:S(2)}) collective-permute-start(f32[256,768]{1,0:T(8,128)} %fusion.7), channel_id=1, source_target_pairs={{0,2},{1,3},{2,0},{3,1},{4,6},{5,7},{6,4},{7,5},{8,10},{9,11},{10,... | collective-permute-start | bytes 2359304 | tf_op jit(solution)/shard_map/ppermute | solution.py:215
  14.1 67.3 %collective-permute-start.8 = (f32[1024,768]{1,0:T(8,128)}, f32[1024,768]{1,0:T(8,128)}, u32[]{:S(2)}, u32[]{:S(2)}) collective-permute-start(f32[1024,768]{1,0:T(8,128)} %fusion.3), channel_id=1, source_target_pairs={{0,1},{1,0},{2,3},{3,2},{4,5},{5,4},{6,7},{7,6},{8,9},{9,8},{10,11... | collective-permute-start | bytes 9437192 | tf_op jit(solution)/shard_map/ppermute | solution.py:215
  35.9 20.5 %collective-permute-start.1 = (f32[256,768]{1,0:T(8,128)S(1)}, f32[256,768]{1,0:T(8,128)}, u32[]{:S(2)}, u32[]{:S(2)}) collective-permute-start(f32[256,768]{1,0:T(8,128)S(1)} %collective-permute-done), channel_id=1, source_target_pairs={{0,4},{4,0},{8,12},{12,8},{1,5},{5,1},{9,13},{13,9},{2,6},{6,2},{1... | collective-permute-start | bytes 2359304 | tf_op jit(solution)/shard_map/ppermute | solution.py:215
  37.7 36.3 %collective-permute-start.2 = (f32[256,768]{1,0:T(8,128)S(1)}, f32[256,768]{1,0:T(8,128)}, u32[]{:S(2)}, u32[]{:S(2)}) collective-permute-start(f32[256,768]{1,0:T(8,128)S(1)} %collective-permute-done), channel_id=1, source_target_pairs={{0,8},{4,12},{8,0},{12,4},{1,9},{5,13},{9,1},{13,5},{2,10},{6,14},... | collective-permute-start | bytes 2359304 | tf_op jit(solution)/shard_map/ppermute | solution.py:215
  39.3 34.8 %collective-permute-start.3 = (f32[256,768]{1,0:T(8,128)S(1)}, f32[256,768]{1,0:T(8,128)}, u32[]{:S(2)}, u32[]{:S(2)}) collective-permute-start(f32[256,768]{1,0:T(8,128)S(1)} %collective-permute-done), channel_id=1, source_target_pairs={{0,12},{4,8},{8,4},{12,0},{1,13},{5,9},{9,5},{13,1},{2,14},{6,10},... | collective-permute-start | bytes 2359304 | tf_op jit(solution)/shard_map/ppermute | solution.py:215
  40.0 40.6 %copy-start.3 = (pred[16,256]{1,0:T(8,128)(4,1)}, pred[16,256]{1,0:T(8,128)(4,1)S(1)}, u32[]{:S(2)}) copy-start(pred[16,256]{1,0:T(8,128)(4,1)S(1)} %broadcast_compare_fusion) | copy-start | bytes 12292
  40.7 37.0 %collective-permute-start.4 = (f32[256,768]{1,0:T(8,128)S(1)}, f32[256,768]{1,0:T(8,128)}, u32[]{:S(2)}, u32[]{:S(2)}) collective-permute-start(f32[256,768]{1,0:T(8,128)S(1)} %collective-permute-done), channel_id=1, source_target_pairs={{0,1},{1,0},{2,3},{3,2},{4,5},{5,4},{6,7},{7,6},{8,9},{9,8},{10,11... | collective-permute-start | bytes 2359304 | tf_op jit(solution)/shard_map/ppermute | solution.py:215
  56.3 21.4 %collective-permute-start.5 = (f32[256,768]{1,0:T(8,128)}, f32[256,768]{1,0:T(8,128)}, u32[]{:S(2)}, u32[]{:S(2)}) collective-permute-start(f32[256,768]{1,0:T(8,128)} %collective-permute-done.1), channel_id=1, source_target_pairs={{0,1},{1,0},{2,3},{3,2},{4,5},{5,4},{6,7},{7,6},{8,9},{9,8},{10,11... | collective-permute-start | bytes 2359304 | tf_op jit(solution)/shard_map/ppermute | solution.py:215
  74.0 3.7 collective-permute-start.6
  74.1 3.6 collective-permute-start.7
  83.8 0.7 copy-start.5
  83.9 0.7 copy-start.13
  258.7 180.1 %collective-permute-start.16 = (f32[6288,768]{1,0:T(8,128)}, f32[6288,768]{1,0:T(8,128)}, u32[]{:S(2)}, u32[]{:S(2)}) collective-permute-start(f32[6288,768]{1,0:T(8,128)} %de_part.1), channel_id=1, source_target_pairs={{0,1},{1,0},{2,3},{3,2},{4,5},{5,4},{6,7},{7,6},{8,9},{9,8},{10,11... | collective-permute-start | bytes 57950216 | tf_op jit(solution)/shard_map/ppermute | solution.py:215
  310.9 2.7 copy-start.1
  313.8 5.6 %collective-permute-start.9 = (f32[4,256,768]{2,1,0:T(8,128)S(1)}, f32[4,256,768]{2,1,0:T(8,128)}, u32[]{:S(2)}, u32[]{:S(2)}) collective-permute-start(f32[4,256,768]{2,1,0:T(8,128)S(1)} %dynamic-slice_bitcast_fusion), channel_id=1, source_target_pairs={{0,1},{1,0},{2,3},{3,2},{4,5},{5,4},{6,7},{7,6},{8,9},{9,8},{10,11... | collective-permute-start | bytes 9437192 | tf_op jit(solution)/shard_map/ppermute | solution.py:215
  322.7 37.1 %copy-start.2 = (f32[4,256,768]{2,1,0:T(8,128)S(1)}, f32[4,256,768]{2,1,0:T(8,128)}, u32[]{:S(2)}) copy-start(f32[4,256,768]{2,1,0:T(8,128)} %convert.5) | copy-start | bytes 9437188
  322.7 37.1 %copy-start.7 = (f32[1,256]{1,0:T(1,128)S(1)}, f32[1,256]{1,0:T(1,128)}, u32[]{:S(2)}) copy-start(f32[1,256]{1,0:T(1,128)} %copy-done.6) | copy-start | bytes 3076
  322.7 37.1 %copy-start.9 = (f32[1,256]{1,0:T(1,128)S(1)}, f32[1,256]{1,0:T(1,128)}, u32[]{:S(2)}) copy-start(f32[1,256]{1,0:T(1,128)} %copy-done.8) | copy-start | bytes 3076
  322.9 20.5 %collective-permute-start.10 = (f32[256,768]{1,0:T(8,128)S(1)}, f32[256,768]{1,0:T(8,128)S(1)}, u32[]{:S(2)}, u32[]{:S(2)}) collective-permute-start(f32[256,768]{1,0:T(8,128)S(1)} %get-tuple-element.40), channel_id=1, source_target_pairs={{0,4},{4,0},{8,12},{12,8},{1,5},{5,1},{9,13},{13,9},{2,6},{6,2},{1... | collective-permute-start | bytes 2359304 | tf_op jit(solution)/shard_map/ppermute | solution.py:215
  323.5 36.2 %collective-permute-start.11 = (f32[256,768]{1,0:T(8,128)S(1)}, f32[256,768]{1,0:T(8,128)S(1)}, u32[]{:S(2)}, u32[]{:S(2)}) collective-permute-start(f32[256,768]{1,0:T(8,128)S(1)} %get-tuple-element.42), channel_id=1, source_target_pairs={{0,8},{4,12},{8,0},{12,4},{1,9},{5,13},{9,1},{13,5},{2,10},{6,14},... | collective-permute-start | bytes 2359304 | tf_op jit(solution)/shard_map/ppermute | solution.py:215
  324.9 39.2 %copy-start.4 = (pred[16,256]{1,0:T(8,128)(4,1)S(1)}, pred[16,256]{1,0:T(8,128)(4,1)}, u32[]{:S(2)}) copy-start(pred[16,256]{1,0:T(8,128)(4,1)} %copy-done.3) | copy-start | bytes 12292
  324.9 39.2 %slice-start = ((pred[16,256]{1,0:T(8,128)(4,1)}), pred[8,256]{1,0:T(8,128)(4,1)S(1)}, s32[]{:S(2)}) async-start(pred[16,256]{1,0:T(8,128)(4,1)} %copy-done.3), calls=%async_computation | async-start | bytes 4096 | tf_op jit(solution)/shard_map/slice | solution.py:294
  324.9 39.2 %copy-start.10 = (f32[4,1,512]{2,1,0:T(1,128)S(1)}, f32[4,1,512]{2,1,0:T(1,128)}, u32[]{:S(2)}) copy-start(f32[4,1,512]{2,1,0:T(1,128)} %get-tuple-element.19) | copy-start | bytes 24580
  324.9 34.8 %collective-permute-start.12 = (f32[256,768]{1,0:T(8,128)S(1)}, f32[256,768]{1,0:T(8,128)S(1)}, u32[]{:S(2)}, u32[]{:S(2)}) collective-permute-start(f32[256,768]{1,0:T(8,128)S(1)} %get-tuple-element.41), channel_id=1, source_target_pairs={{0,12},{4,8},{8,4},{12,0},{1,13},{5,9},{9,5},{13,1},{2,14},{6,10},... | collective-permute-start | bytes 2359304 | tf_op jit(solution)/shard_map/ppermute | solution.py:215
  360.6 76.0 %collective-permute-start.13 = (f32[256,768]{1,0:T(8,128)S(1)}, f32[256,768]{1,0:T(8,128)S(1)}, u32[]{:S(2)}, u32[]{:S(2)}) collective-permute-start(f32[256,768]{1,0:T(8,128)S(1)} %multiply_subtract_fusion), channel_id=1, source_target_pairs={{0,4},{4,0},{8,12},{12,8},{1,5},{5,1},{9,13},{13,9},{2,6},{6,2},{1... | collective-permute-start | bytes 2359304 | tf_op jit(solution)/shard_map/ppermute | solution.py:215
  362.0 74.5 %collective-permute-start.14 = (f32[256,768]{1,0:T(8,128)S(1)}, f32[256,768]{1,0:T(8,128)S(1)}, u32[]{:S(2)}, u32[]{:S(2)}) collective-permute-start(f32[256,768]{1,0:T(8,128)S(1)} %multiply_subtract_fusion), channel_id=1, source_target_pairs={{0,8},{4,12},{8,0},{12,4},{1,9},{5,13},{9,1},{13,5},{2,10},{6,14},... | collective-permute-start | bytes 2359304 | tf_op jit(solution)/shard_map/ppermute | solution.py:215
  362.6 73.9 %collective-permute-start.15 = (f32[256,768]{1,0:T(8,128)S(1)}, f32[256,768]{1,0:T(8,128)S(1)}, u32[]{:S(2)}, u32[]{:S(2)}) collective-permute-start(f32[256,768]{1,0:T(8,128)S(1)} %multiply_subtract_fusion), channel_id=1, source_target_pairs={{0,12},{4,8},{8,4},{12,0},{1,13},{5,9},{9,5},{13,1},{2,14},{6,10},... | collective-permute-start | bytes 2359304 | tf_op jit(solution)/shard_map/ppermute | solution.py:215
